TPU v7x, 32 devices: a whole 2x2x4 slice. The times are simulated.
32 devices in a mesh: dp: 8 (over z, core), mp: 4 (over y, x).
Axes of the slice: x: 2, y: 2, z: 4, core: 2. Of those that a mesh axis runs over, the one named last changes fastest.
Arguments:
- features: bfloat16 [8192, 8192], P('dp', 'mp'), may hold values from -6 to 6
- v_weight: bfloat16 [3, 8192, 1024], P(None, 'mp', 'dp'), may hold values from -0.0625 to 0.0625
- u_weight: bfloat16 [3, 1024, 8192], P(None, 'dp', 'mp'), may hold values from -0.1875 to 0.1875
- cross_bias: float32 [3, 8192], P(None, 'mp'), may hold values from -3 to 3
Outputs:
- crossed: bfloat16 [8192, 8192], P('dp', 'mp')
All inputs are finite; a program needn't handle non-finite values.
Results may differ from a plain program's by a relative error of at most 0.009.
Values may be sent and summed in bfloat16 or wider, within the bound.
A program may use at most 128 MiB of HBM per device.

v0:
```python
import jax
import jax.numpy as jnp
from jax import lax
from jax.sharding import PartitionSpec as P


def local(features, v_weight, u_weight, cross_bias):
    carried = features
    layers = v_weight.shape[0]
    for layer_number in range(layers):
        current = carried
        partial_value = jnp.dot(
            current,
            lax.all_gather(v_weight[layer_number], "dp", axis=1, tiled=True),
            preferred_element_type=jnp.float32,
        )
        rank_proj = lax.psum(partial_value, "mp").astype(jnp.bfloat16)
        cross_term = jnp.dot(
            rank_proj,
            lax.all_gather(u_weight[layer_number], "dp", axis=0, tiled=True),
            preferred_element_type=jnp.float32,
        )
        cross_term = cross_term + cross_bias[layer_number]
        carried = (features.astype(jnp.float32) * cross_term + current.astype(jnp.float32)).astype(
            jnp.bfloat16
        )
    return carried


def solution(mesh):
    return jax.shard_map(
        local,
        mesh=mesh,
        in_specs=(P("dp", "mp"), P(None, "mp", "dp"), P(None, "dp", "mp"), P(None, "mp")),
        out_specs=P("dp", "mp"),
        check_vma=False,
    )
```

profile of v0, /device:TPU:0, one launch (start us, length us, event | category | flops | bytes accessed | tf_op | source)
XLA Modules:
  0.0 553.8 jit_solution(13807894456703240402)
XLA Ops:
  6.5 0.0 copy-start
  6.5 0.0 copy-start.1
  6.5 0.0 all-gather.13.cloned.1.call-start
  6.5 2.6 fusion.26
  9.2 0.0 all-gather.13.cloned.1.call-update
  9.2 0.0 all-gather.15.cloned.1.call-start
  9.3 0.0 copy-done
  9.3 1.2 fusion.27
  10.5 0.0 all-gather.15.cloned.1.call-update
  10.5 0.0 all-gather.17.cloned.1.call-start
  10.6 0.7 all-gather.17.cloned.1.call-update
  11.2 0.0 all-gather.19.cloned.1.call-start
  11.3 0.5 all-gather.19.cloned.1.call-update
  11.8 0.0 all-gather.21.cloned.1.call-start
  11.9 0.5 all-gather.21.cloned.1.call-update
  12.4 0.0 all-gather.23.cloned.1.call-start
  12.5 0.5 all-gather.23.cloned.1.call-update
  13.0 0.0 copy-done.1
  13.0 46.9 %all-gather.13.cloned.1.call-done = bf16[1,2048,1024]{2,1,0:T(8,128)(2,1)} async-done(((bf16[1,2048,128]{2,1,0:T(8,128)(2,1)}), bf16[1,2048,1024]{2,1,0:T(8,128)(2,1)}) %all-gather.13.cloned.1.call-update) | async-done | bytes 4194320 | tf_op jit(solution)/shard_map/all_gather | solution.py:14
  59.9 10.0 %fusion.15 = f32[1024,1024]{1,0:T(8,128)} fusion(bf16[1024,2048]{1,0:T(8,128)(2,1)} %param.4, bf16[1,2048,1024]{2,1,0:T(8,128)(2,1)} %all-gather.13.cloned.1.call-done), kind=kOutput, calls=%fused_computation.19 | convolution fusion | flops 4294967296 | bytes 12582912 | tf_op jit(solution)/shard_map/dot_general | solution.py:12
  69.9 145.6 %all-reduce.3 = bf16[1024,1024]{1,0:T(8,128)(2,1)S(1)} all-reduce(f32[1024,1024]{1,0:T(8,128)} %fusion.15), channel_id=1, replica_groups=mesh['dp'=8,'mp'=4] {'mp'}, use_global_device_ids=true, to_apply=%region_0.0 | all-reduce | flops 1048576 | bytes 6291456 | tf_op jit(solution)/shard_map/psum | solution.py:17
  215.5 0.0 all-gather.15.cloned.1.call-done
  215.6 9.2 %fusion = bf16[1024,2048]{1,0:T(8,128)(2,1)} fusion(bf16[1024,2048]{1,0:T(8,128)(2,1)} %param.4, f32[2048]{0:T(1024)S(1)} %bitcast.35, bf16[1,1024,2048]{2,1,0:T(8,128)(2,1)} %all-gather.15.cloned.1.call-done, bf16[1024,1024]{1,0:T(8,128)(2,1)S(1)} %all-reduce.3), kind=kOutput, calls=%fused_computation.4 | convolution fusion | flops 4305453056 | bytes 14688256 | tf_op jit(solution)/shard_map/dot_general | solution.py:18
  224.8 0.0 all-gather.17.cloned.1.call-done
  224.8 10.0 %fusion.11 = f32[1024,1024]{1,0:T(8,128)} fusion(bf16[1024,2048]{1,0:T(8,128)(2,1)} %fusion, bf16[1,2048,1024]{2,1,0:T(8,128)(2,1)} %all-gather.17.cloned.1.call-done), kind=kOutput, calls=%fused_computation.15 | convolution fusion | flops 4294967296 | bytes 12582912 | tf_op jit(solution)/shard_map/dot_general | solution.py:12
  234.8 142.2 %all-reduce.4 = bf16[1024,1024]{1,0:T(8,128)(2,1)S(1)} all-reduce(f32[1024,1024]{1,0:T(8,128)} %fusion.11), channel_id=1, replica_groups=mesh['dp'=8,'mp'=4] {'mp'}, use_global_device_ids=true, to_apply=%region_1.0 | all-reduce | flops 1048576 | bytes 6291456 | tf_op jit(solution)/shard_map/psum | solution.py:17
  377.1 0.0 all-gather.19.cloned.1.call-done
  377.1 9.9 %fusion.2 = bf16[1024,2048]{1,0:T(8,128)(2,1)} fusion(bf16[1024,2048]{1,0:T(8,128)(2,1)} %param.4, bf16[1024,2048]{1,0:T(8,128)(2,1)} %fusion, f32[2048]{0:T(1024)S(1)} %bitcast.34, bf16[1,1024,2048]{2,1,0:T(8,128)(2,1)} %all-gather.19.cloned.1.call-done, bf16[1024,1024]{1,0:T(8,128)(2,1)S(1)} %all-reduce.4), kind=kOutput, calls=%fused_computation.6 | convolution fusion | flops 4307550208 | bytes 18882560 | tf_op jit(solution)/shard_map/dot_general | solution.py:18
  387.0 0.0 all-gather.21.cloned.1.call-done
  387.0 9.9 %fusion.7 = f32[1024,1024]{1,0:T(8,128)} fusion(bf16[1024,2048]{1,0:T(8,128)(2,1)} %fusion.2, bf16[1,2048,1024]{2,1,0:T(8,128)(2,1)} %all-gather.21.cloned.1.call-done), kind=kOutput, calls=%fused_computation.11 | convolution fusion | flops 4294967296 | bytes 12582912 | tf_op jit(solution)/shard_map/dot_general | solution.py:12
  396.9 140.1 %all-reduce.5 = bf16[1024,1024]{1,0:T(8,128)(2,1)S(1)} all-reduce(f32[1024,1024]{1,0:T(8,128)} %fusion.7), channel_id=1, replica_groups=mesh['dp'=8,'mp'=4] {'mp'}, use_global_device_ids=true, to_apply=%region_2.0 | all-reduce | flops 1048576 | bytes 6291456 | tf_op jit(solution)/shard_map/psum | solution.py:17
  537.0 0.0 all-gather.23.cloned.1.call-done
  537.1 9.9 %fusion.4 = bf16[1024,2048]{1,0:T(8,128)(2,1)} fusion(bf16[1024,2048]{1,0:T(8,128)(2,1)} %param.4, bf16[1024,2048]{1,0:T(8,128)(2,1)} %fusion.2, f32[2048]{0:T(1024)S(1)} %bitcast.33, bf16[1,1024,2048]{2,1,0:T(8,128)(2,1)} %all-gather.23.cloned.1.call-done, bf16[1024,1024]{1,0:T(8,128)(2,1)S(1)} %all-reduce.5), kind=kOutput, calls=%fused_computation.8 | convolution fusion | flops 4307550208 | bytes 18882560 | tf_op jit(solution)/shard_map/dot_general | solution.py:18
  (1 shorter events, 0.0 us)
Async XLA Ops:
  6.5 2.7 copy-start
  6.5 6.4 %copy-start.1 = (f32[3,2048]{1,0:T(4,128)S(1)}, f32[3,2048]{1,0:T(4,128)}, u32[]{:S(2)}) copy-start(f32[3,2048]{1,0:T(4,128)} %param.7) | copy-start | bytes 73732
  6.5 53.4 %all-gather.13.cloned.1.call-start = ((), (), s32[]{:S(2)}) async-start(), calls=%async_computation | async-start | bytes 4718592 | tf_op jit(solution)/shard_map/all_gather | solution.py:14
  9.2 206.3 %all-gather.15.cloned.1.call-start = ((), (), s32[]{:S(2)}) async-start(), calls=%async_computation.1 | async-start | bytes 4718592 | tf_op jit(solution)/shard_map/all_gather | solution.py:20
  10.5 214.3 %all-gather.17.cloned.1.call-start = ((), (), s32[]{:S(2)}) async-start(), calls=%async_computation.2 | async-start | bytes 4718592 | tf_op jit(solution)/shard_map/all_gather | solution.py:14
  11.2 365.8 %all-gather.19.cloned.1.call-start = ((), (), s32[]{:S(2)}) async-start(), calls=%async_computation.3 | async-start | bytes 4718592 | tf_op jit(solution)/shard_map/all_gather | solution.py:20
  11.8 375.1 %all-gather.21.cloned.1.call-start = ((), (), s32[]{:S(2)}) async-start(), calls=%async_computation.4 | async-start | bytes 4718592 | tf_op jit(solution)/shard_map/all_gather | solution.py:14
  12.4 524.6 %all-gather.23.cloned.1.call-start = ((), (), s32[]{:S(2)}) async-start(), calls=%async_computation.5 | async-start | bytes 4718592 | tf_op jit(solution)/shard_map/all_gather | solution.py:20
Sparse Core Ops, SparseCore 0:
  9.3 50.5 all-gather.12
  61.5 45.0 all-gather.14
  108.2 46.6 all-gather.16
  156.3 45.0 all-gather.18
  202.8 46.6 all-gather.20
  250.9 45.0 all-gather.22
where the time goes:
time: 554 us
  blocking collectives  428 us (77%)
  matrix products  58.9 us (11%)
  waiting for transfers between devices  49.3 us (9%)
  between operations  13.5 us (2%)
    psum x3, blocking collectives, local(): rank_proj = lax.psum(partial_value, 'mp').astype(jnp.bfloat16)  428 us
    all_gather x3, waiting for transfers between devices, local(): lax.all_gather(v_weight[layer_number], 'dp', axis=1, tiled=True)  46.9 us
    dot_general x3, matrix products, local(): jnp.dot(current, lax.all_gather(v_weight[layer_number], 'dp', axis=1, til...  29.9 us
    dot_general x3, matrix products, local(): jnp.dot(rank_proj, lax.all_gather(u_weight[layer_number], 'dp', axis=0, t...  29 us
  transfers between devices with their start and end apart: 6, of which 1 were waited for; matrix products, arithmetic and copies ran while one was open for 9% of the time, Pallas kernels for 0%

commit v1 on v0

--- a/solution.py
+++ b/solution.py
@@ -14,7 +14,7 @@
             lax.all_gather(v_weight[layer_number], "dp", axis=1, tiled=True),
             preferred_element_type=jnp.float32,
         )
-        rank_proj = lax.psum(partial_value, "mp").astype(jnp.bfloat16)
+        rank_proj = jnp.sum(lax.all_gather(partial_value, "mp"), axis=0).astype(jnp.bfloat16)
         cross_term = jnp.dot(
             rank_proj,
             lax.all_gather(u_weight[layer_number], "dp", axis=0, tiled=True),

time: 554 us -> 815 us (1.47)
  waiting for transfers between devices: 49.3 us -> 712 us
  blocking collectives: 428 us -> 0 us
  other arithmetic: 0 us -> 25 us
    all_gather x0 -> x3, waiting for transfers between devices: none -> 461 us  [local(): lax.all_gather(partial_value, 'mp')]
    psum x3 -> x0, blocking collectives: 428 us -> none  [local(): rank_proj = lax.psum(partial_value, 'mp').astype(jnp.bfloat16)]
    all_gather x3, waiting for transfers between devices: 0.06 us -> 120 us  [local(): lax.all_gather(u_weight[layer_number], 'dp', axis=0, tiled=True)]
    all_gather x3, waiting for transfers between devices: 46.9 us -> 128 us  [local(): lax.all_gather(v_weight[layer_number], 'dp', axis=1, tiled=True)]
    reduce_sum x0 -> x3, other arithmetic: none -> 25 us  [local(): jnp.sum(lax.all_gather(partial_value, 'mp'), axis=0).astype(jnp.bfloat16)]
  transfers between devices with their start and end apart: 6 -> 9, of which waited for: 1 -> 9; matrix products, arithmetic and copies ran while one was open for 9% -> 6% of each run, Pallas kernels for 0% -> 0%
where the time goes in v1:
time: 815 us
  waiting for transfers between devices  712 us (87%)
  matrix products  58.9 us (7%)
  other arithmetic  25 us (3%)
  between operations  13.3 us (2%)
    all_gather x3, waiting for transfers between devices, local(): lax.all_gather(partial_value, 'mp')  461 us
    all_gather x3, waiting for transfers between devices, local(): lax.all_gather(v_weight[layer_number], 'dp', axis=1, tiled=True)  128 us
    all_gather x3, waiting for transfers between devices, local(): lax.all_gather(u_weight[layer_number], 'dp', axis=0, tiled=True)  120 us
    dot_general x3, matrix products, local(): jnp.dot(current, lax.all_gather(v_weight[layer_number], 'dp', axis=1, til...  29.8 us
    dot_general x3, matrix products, local(): jnp.dot(rank_proj, lax.all_gather(u_weight[layer_number], 'dp', axis=0, t...  29.1 us
    reduce_sum x3, other arithmetic, local(): jnp.sum(lax.all_gather(partial_value, 'mp'), axis=0).astype(jnp.bfloat16)  25 us
  transfers between devices with their start and end apart: 9, of which 9 were waited for; matrix products, arithmetic and copies ran while one was open for 6% of the time, Pallas kernels for 0%

profile of v1, /device:TPU:0, one launch (start us, length us, event | category | flops | bytes accessed | tf_op | source)
XLA Modules:
  0.0 814.8 jit_solution(11563156104398451564)
XLA Ops:
  6.5 0.0 all-gather.19.cloned.1.call-start
  6.5 2.6 fusion.26
  9.1 0.0 all-gather.19.cloned.1.call-update
  9.1 0.0 all-gather.21.cloned.1.call-start
  9.2 50.6 %all-gather.19.cloned.1.call-done = bf16[1,2048,1024]{2,1,0:T(8,128)(2,1)} async-done(((bf16[1,2048,128]{2,1,0:T(8,128)(2,1)}), bf16[1,2048,1024]{2,1,0:T(8,128)(2,1)}) %all-gather.19.cloned.1.call-update) | async-done | bytes 4194320 | tf_op jit(solution)/shard_map/all_gather | solution.py:14
  59.8 10.0 %fusion.15 = f32[1024,1024]{1,0:T(8,128)} fusion(bf16[1024,2048]{1,0:T(8,128)(2,1)} %param.4, bf16[1,2048,1024]{2,1,0:T(8,128)(2,1)} %all-gather.19.cloned.1.call-done), kind=kOutput, calls=%fused_computation.19 | convolution fusion | flops 4294967296 | bytes 12582912 | tf_op jit(solution)/shard_map/dot_general | solution.py:12
  69.8 0.0 copy-start
  69.8 0.0 copy-start.1
  69.8 0.0 all-gather.21.cloned.1.call-update
  69.8 0.0 all-gather.23.cloned.1.call-start
  69.9 1.3 copy-done
  71.2 1.2 fusion.27
  72.5 0.0 all-gather.23.cloned.1.call-update
  72.5 0.0 all-gather.25.cloned.1.call-start
  72.5 0.5 all-gather.25.cloned.1.call-update
  73.1 0.0 all-gather.27.cloned.1.call-start
  73.1 0.0 copy-done.1
  73.1 152.3 %all-gather.21.cloned.1.call-done = f32[4096,1024]{1,0:T(8,128)} async-done(((f32[1024,1024]{1,0:T(8,128)}), f32[4096,1024]{1,0:T(8,128)}) %all-gather.21.cloned.1.call-update) | async-done | bytes 16777232 | tf_op jit(solution)/shard_map/all_gather | solution.py:17
  225.5 8.3 %reduce_sum.27 = bf16[1024,1024]{1,0:T(8,128)(2,1)S(1)} reduce(f32[4,1024,1024]{2,1,0:T(8,128)} %bitcast.36, f32[]{:T(128)} %constant.0.clone.1), dimensions={0}, to_apply=%region_0.0 | reduce | flops 3145728 | bytes 18874372 | tf_op jit(solution)/shard_map/reduce_sum | solution.py:17
  233.8 40.2 %all-gather.23.cloned.1.call-done = bf16[1,1024,2048]{2,1,0:T(8,128)(2,1)} async-done(((bf16[1,128,2048]{2,1,0:T(8,128)(2,1)}), bf16[1,1024,2048]{2,1,0:T(8,128)(2,1)}) %all-gather.23.cloned.1.call-update) | async-done | bytes 4194320 | tf_op jit(solution)/shard_map/all_gather | solution.py:20
  274.0 9.3 %fusion = bf16[1024,2048]{1,0:T(8,128)(2,1)} fusion(bf16[1024,2048]{1,0:T(8,128)(2,1)} %param.4, f32[2048]{0:T(1024)S(1)} %bitcast.41, bf16[1,1024,2048]{2,1,0:T(8,128)(2,1)} %all-gather.23.cloned.1.call-done, bf16[1024,1024]{1,0:T(8,128)(2,1)S(1)} %reduce_sum.27), kind=kOutput, calls=%fused_computation.4 | convolution fusion | flops 4305453056 | bytes 14688256 | tf_op jit(solution)/shard_map/dot_general | solution.py:18
  283.3 38.8 %all-gather.25.cloned.1.call-done = bf16[1,2048,1024]{2,1,0:T(8,128)(2,1)} async-done(((bf16[1,2048,128]{2,1,0:T(8,128)(2,1)}), bf16[1,2048,1024]{2,1,0:T(8,128)(2,1)}) %all-gather.25.cloned.1.call-update) | async-done | bytes 4194320 | tf_op jit(solution)/shard_map/all_gather | solution.py:14
  322.1 9.9 %fusion.11 = f32[1024,1024]{1,0:T(8,128)} fusion(bf16[1024,2048]{1,0:T(8,128)(2,1)} %fusion, bf16[1,2048,1024]{2,1,0:T(8,128)(2,1)} %all-gather.25.cloned.1.call-done), kind=kOutput, calls=%fused_computation.15 | convolution fusion | flops 4294967296 | bytes 12582912 | tf_op jit(solution)/shard_map/dot_general | solution.py:12
  332.0 0.0 all-gather.27.cloned.1.call-update
  332.0 0.0 all-gather.29.cloned.1.call-start
  332.1 0.5 all-gather.29.cloned.1.call-update
  332.6 0.0 all-gather.31.cloned.1.call-start
  332.7 0.7 all-gather.31.cloned.1.call-update
  333.4 0.2 all-gather.33.cloned.1.call-start
  333.6 154.1 %all-gather.27.cloned.1.call-done = f32[4096,1024]{1,0:T(8,128)} async-done(((f32[1024,1024]{1,0:T(8,128)}), f32[4096,1024]{1,0:T(8,128)}) %all-gather.27.cloned.1.call-update) | async-done | bytes 16777232 | tf_op jit(solution)/shard_map/all_gather | solution.py:17
  487.7 8.3 %reduce_sum.28 = bf16[1024,1024]{1,0:T(8,128)(2,1)S(1)} reduce(f32[4,1024,1024]{2,1,0:T(8,128)} %bitcast.37, f32[]{:T(128)} %constant.0.clone.1), dimensions={0}, to_apply=%region_1.0 | reduce | flops 3145728 | bytes 18874372 | tf_op jit(solution)/shard_map/reduce_sum | solution.py:17
  496.0 40.0 %all-gather.29.cloned.1.call-done = bf16[1,1024,2048]{2,1,0:T(8,128)(2,1)} async-done(((bf16[1,128,2048]{2,1,0:T(8,128)(2,1)}), bf16[1,1024,2048]{2,1,0:T(8,128)(2,1)}) %all-gather.29.cloned.1.call-update) | async-done | bytes 4194320 | tf_op jit(solution)/shard_map/all_gather | solution.py:20
  536.0 9.9 %fusion.2 = bf16[1024,2048]{1,0:T(8,128)(2,1)} fusion(bf16[1024,2048]{1,0:T(8,128)(2,1)} %param.4, bf16[1024,2048]{1,0:T(8,128)(2,1)} %fusion, f32[2048]{0:T(1024)S(1)} %bitcast.40, bf16[1,1024,2048]{2,1,0:T(8,128)(2,1)} %all-gather.29.cloned.1.call-done, bf16[1024,1024]{1,0:T(8,128)(2,1)S(1)} %reduce_sum.28), kind=kOutput, calls=%fused_computation.6 | convolution fusion | flops 4307550208 | bytes 18882560 | tf_op jit(solution)/shard_map/dot_general | solution.py:18
  545.9 38.4 %all-gather.31.cloned.1.call-done = bf16[1,2048,1024]{2,1,0:T(8,128)(2,1)} async-done(((bf16[1,2048,128]{2,1,0:T(8,128)(2,1)}), bf16[1,2048,1024]{2,1,0:T(8,128)(2,1)}) %all-gather.31.cloned.1.call-update) | async-done | bytes 4194320 | tf_op jit(solution)/shard_map/all_gather | solution.py:14
  584.3 10.0 %fusion.7 = f32[1024,1024]{1,0:T(8,128)} fusion(bf16[1024,2048]{1,0:T(8,128)(2,1)} %fusion.2, bf16[1,2048,1024]{2,1,0:T(8,128)(2,1)} %all-gather.31.cloned.1.call-done), kind=kOutput, calls=%fused_computation.11 | convolution fusion | flops 4294967296 | bytes 12582912 | tf_op jit(solution)/shard_map/dot_general | solution.py:12
  594.2 0.0 all-gather.33.cloned.1.call-update
  594.2 0.3 all-gather.35.cloned.1.call-start
  594.5 0.5 all-gather.35.cloned.1.call-update
  595.0 154.9 %all-gather.33.cloned.1.call-done = f32[4096,1024]{1,0:T(8,128)} async-done(((f32[1024,1024]{1,0:T(8,128)}), f32[4096,1024]{1,0:T(8,128)}) %all-gather.33.cloned.1.call-update) | async-done | bytes 16777232 | tf_op jit(solution)/shard_map/all_gather | solution.py:17
  749.9 8.3 %reduce_sum.29 = bf16[1024,1024]{1,0:T(8,128)(2,1)S(1)} reduce(f32[4,1024,1024]{2,1,0:T(8,128)} %bitcast.38, f32[]{:T(128)} %constant.0.clone.1), dimensions={0}, to_apply=%region_2.0 | reduce | flops 3145728 | bytes 18874372 | tf_op jit(solution)/shard_map/reduce_sum | solution.py:17
  758.2 40.2 %all-gather.35.cloned.1.call-done = bf16[1,1024,2048]{2,1,0:T(8,128)(2,1)} async-done(((bf16[1,128,2048]{2,1,0:T(8,128)(2,1)}), bf16[1,1024,2048]{2,1,0:T(8,128)(2,1)}) %all-gather.35.cloned.1.call-update) | async-done | bytes 4194320 | tf_op jit(solution)/shard_map/all_gather | solution.py:20
  798.4 9.9 %fusion.4 = bf16[1024,2048]{1,0:T(8,128)(2,1)} fusion(bf16[1024,2048]{1,0:T(8,128)(2,1)} %param.4, bf16[1024,2048]{1,0:T(8,128)(2,1)} %fusion.2, f32[2048]{0:T(1024)S(1)} %bitcast.39, bf16[1,1024,2048]{2,1,0:T(8,128)(2,1)} %all-gather.35.cloned.1.call-done, bf16[1024,1024]{1,0:T(8,128)(2,1)S(1)} %reduce_sum.29), kind=kOutput, calls=%fused_computation.8 | convolution fusion | flops 4307550208 | bytes 18882560 | tf_op jit(solution)/shard_map/dot_general | solution.py:18
  (1 shorter events, 0.0 us)
Async XLA Ops:
  6.5 53.3 %all-gather.19.cloned.1.call-start = ((), (), s32[]{:S(2)}) async-start(), calls=%async_computation | async-start | bytes 4718592 | tf_op jit(solution)/shard_map/all_gather | solution.py:14
  9.1 216.3 %all-gather.21.cloned.1.call-start = ((), (), s32[]{:S(2)}) async-start(), calls=%async_computation.1 | async-start | bytes 20971520 | tf_op jit(solution)/shard_map/all_gather | solution.py:17
  69.8 1.4 copy-start
  69.8 3.3 copy-start.1
  69.8 204.1 %all-gather.23.cloned.1.call-start = ((), (), s32[]{:S(2)}) async-start(), calls=%async_computation.2 | async-start | bytes 4718592 | tf_op jit(solution)/shard_map/all_gather | solution.py:20
  72.5 249.6 %all-gather.25.cloned.1.call-start = ((), (), s32[]{:S(2)}) async-start(), calls=%async_computation.3 | async-start | bytes 4718592 | tf_op jit(solution)/shard_map/all_gather | solution.py:14
  73.1 414.6 %all-gather.27.cloned.1.call-start = ((), (), s32[]{:S(2)}) async-start(), calls=%async_computation.4 | async-start | bytes 20971520 | tf_op jit(solution)/shard_map/all_gather | solution.py:17
  332.0 204.0 %all-gather.29.cloned.1.call-start = ((), (), s32[]{:S(2)}) async-start(), calls=%async_computation.5 | async-start | bytes 4718592 | tf_op jit(solution)/shard_map/all_gather | solution.py:20
  332.6 251.6 %all-gather.31.cloned.1.call-start = ((), (), s32[]{:S(2)}) async-start(), calls=%async_computation.6 | async-start | bytes 4718592 | tf_op jit(solution)/shard_map/all_gather | solution.py:14
  333.4 416.5 %all-gather.33.cloned.1.call-start = ((), (), s32[]{:S(2)}) async-start(), calls=%async_computation.7 | async-start | bytes 20971520 | tf_op jit(solution)/shard_map/all_gather | solution.py:17
  594.2 204.1 %all-gather.35.cloned.1.call-start = ((), (), s32[]{:S(2)}) async-start(), calls=%async_computation.8 | async-start | bytes 4718592 | tf_op jit(solution)/shard_map/all_gather | solution.py:20
Sparse Core Ops, SparseCore 0:
  9.3 50.5 all-gather.18
  70.0 155.4 all-gather.20
  227.1 46.8 all-gather.22
  275.4 46.6 all-gather.24
  332.2 155.4 all-gather.26
  489.1 46.8 all-gather.28
  537.6 46.6 all-gather.30
  594.4 155.4 all-gather.32
  751.5 46.8 all-gather.34
